TPU v7x, 256 devices: a whole 4x4x8 slice. The times are simulated.
256 devices in a mesh: blk: 64 (over x, y_lo, z), grp: 4 (over y_hi, core).
Axes of the slice: x: 4, y: 4 (y_hi: 2, y_lo: 2; y = y_hi * 2 + y_lo), z: 8, core: 2. Of those that a mesh axis runs over, the one named last changes fastest.
Arguments:
- sources: bfloat16 [65536, 256], P('blk'), may hold values from -64 to 64
- positive: int32 [65536], P('blk'), may hold values from 0 to 65535
- src_part: int32 [65536], P('blk'), may hold values from 0 to 7
- destinations: bfloat16 [65536, 256], P(('blk', 'grp')), may hold values from -8 to 8
- dst_part: int32 [65536], P(('blk', 'grp')), may hold values from 0 to 7
Outputs:
- loss: float32 [65536], P('blk')
All inputs are finite; a program needn't handle non-finite values.
Results may differ from a plain program's by a relative error of at most 0.0003.
Values may be sent and summed in bfloat16 or wider, within the bound.
A program may use at most 192 MiB of HBM per device.

v0:
```python
import jax
import jax.numpy as jnp
from jax import lax
from jax.sharding import Mesh
from jax.sharding import PartitionSpec as P

BLK = ("blk_0", "blk_1", "blk_2")
BLK_GRP = ("blk_0", "blk_1", "blk_2", "grp")
SCALE = 3.0
NEG = -1e30


def joined_along(parts, dim):
    dims = list(parts.shape[1:])
    dims[dim] *= parts.shape[0]
    return jnp.moveaxis(parts, 0, dim).reshape(dims)


def stacked_from(x, axes, order):
    parts = x[None]
    for k in order:
        parts = lax.all_gather(parts, axes[k], axis=0, tiled=True)
    held = [lax.axis_size(axes[k]) for k in reversed(order)]
    parts = parts.reshape(*held, *x.shape)
    turned = sorted(range(len(order)), key=lambda place: order[len(order) - 1 - place])
    return parts.transpose(*turned, *range(len(order), parts.ndim)).reshape(-1, *x.shape)


def whole_of(x, axes, order, dim):
    return joined_along(stacked_from(x, axes, order), dim)


def copy_for_each(x, axis):
    size = lax.axis_size(axis)
    return lax.all_to_all(jnp.broadcast_to(x[None], (size, *x.shape)), axis, 0, 0, tiled=True)


def collected_together(x, axis):
    leaves = jax.tree.leaves(x)
    order = sorted(range(len(leaves)), key=lambda k: -leaves[k].size)
    width = (1, *leaves[order[0]].shape)[-1]
    lines = [
        jnp.pad(leaves[k].reshape(-1), (0, -leaves[k].size % width)).reshape(-1, width)
        for k in order
    ]
    both, at, found = (copy_for_each(jnp.concatenate(lines), axis), 0, {})
    for k, line in zip(order, lines):
        section = both[:, at : at + len(line)].reshape(len(both), -1)
        found[k] = section[:, : leaves[k].size].reshape(-1, *leaves[k].shape)
        at += len(line)
    numbers = iter(range(len(leaves)))
    return jax.tree.map(lambda _: found[next(numbers)], x)


def combined_pairwise(pieces, combine):
    while len(jax.tree.leaves(pieces)[0]) > 1:
        pieces = jax.vmap(combine)(
            *(jax.tree.map(lambda part: part[side::2], pieces) for side in (0, 1))
        )
    return jax.tree.map(lambda part: part[0], pieces)


def joined_all(x, axis, combine):
    pieces = collected_together(x, axis)
    return combined_pairwise(pieces, combine)


def global_columns(count, width, group, groups):
    flat = jnp.arange(count, dtype=jnp.int32)
    return flat // width * (groups * width) + group * width + flat % width


def score_block(carry, sources, positive, src_part, block, block_part, columns):
    maxima, totals, pos_logit = carry
    logits = SCALE * lax.dot_general(
        sources, block, (((1,), (1,)), ((), ())), preferred_element_type=jnp.float32
    )
    is_pos = columns[None, :] == positive[:, None]
    keep = (block_part[None, :] != src_part[:, None]) | is_pos
    masked = jnp.where(keep, logits, NEG)
    new_max = jnp.maximum(maxima, jnp.max(masked, axis=1))
    weights = jnp.where(keep, jnp.exp(masked - new_max[:, None]), 0.0)
    totals = jnp.sum(weights, axis=1)
    pos_logit = jnp.sum(jnp.where(is_pos, logits, 0.0), axis=1)
    return (new_max, totals, pos_logit)


def combine(first, second):
    max_a, sum_a, pos_a = first
    max_b, sum_b, pos_b = second
    top = jnp.maximum(max_a, max_b)
    return (top, sum_a * jnp.exp(max_a - top) + sum_b * jnp.exp(max_b - top), pos_a + pos_b)


def on_device(sources, positive, src_part, destinations, dst_part):
    width = destinations.shape[0]
    count_rows = sources.shape[0]
    groups = lax.axis_size("grp")
    group = lax.axis_index("grp")
    start = (
        jnp.full((count_rows,), NEG, jnp.float32),
        jnp.zeros((count_rows,), jnp.float32),
        jnp.zeros((count_rows,), jnp.float32),
    )
    block = whole_of(destinations, BLK, (1, 0, 2), 0)
    columns = global_columns(block.shape[0], width, group, groups)
    carry = score_block(
        start, sources, positive, src_part, block, whole_of(dst_part, BLK, (1, 0, 2), 0), columns
    )
    maxima, totals, pos_logit = joined_all(carry, "grp", combine)
    return maxima + jnp.log(totals) - pos_logit


def solution(mesh):
    finer = Mesh(
        mesh.devices.reshape(4, 2, 8, mesh.shape["grp"]), ("blk_0", "blk_1", "blk_2", "grp")
    )
    placed = (P(BLK, None), P(BLK), P(BLK), P(BLK_GRP, None), P(BLK_GRP))
    return jax.shard_map(on_device, mesh=finer, in_specs=placed, out_specs=P(BLK), check_vma=False)
```

profile of v0, /device:TPU:1, one launch (start us, length us, event | category | flops | bytes accessed | tf_op | source)
XLA Modules:
  0.0 231.4 jit_solution(11904566351215980522)
XLA Ops:
  6.5 0.0 copy-start
  6.5 0.0 all-gather.7.cloned.1.call-start
  6.5 7.1 %all-gather.1 = bf16[512,256]{1,0:T(8,128)(2,1)} all-gather(bf16[256,256]{1,0:T(8,128)(2,1)} %param.8), channel_id=3, replica_groups=mesh['blk_0'=4,'blk_1'=2,'blk_2'=8,'grp'=4] {'blk_1'}, dimensions={0}, use_global_device_ids=true | all-gather | bytes 393216 | tf_op jit(solution)/shard_map/all_gather | solution.py:22
  13.7 0.0 all-gather.7.cloned.1.call-update
  13.7 0.0 all-gather.9.cloned.1.call-start
  13.7 28.8 %all-gather.7.cloned.1.call-done = bf16[8,256,256]{2,1,0:T(8,128)(2,1)} async-done(((bf16[2,256,256]{2,1,0:T(8,128)(2,1)}), bf16[8,256,256]{2,1,0:T(8,128)(2,1)}) %all-gather.7.cloned.1.call-update) | async-done | bytes 1048592 | tf_op jit(solution)/shard_map/all_gather | solution.py:22
  42.5 0.0 all-gather.9.cloned.1.call-update
  42.5 3.3 %all-gather.2 = s32[2,1,256]{2,1,0:T(1,128)S(1)} all-gather(s32[1,1,256]{2,1,0:T(1,128)} %bitcast.35), channel_id=2, replica_groups=mesh['blk_0'=4,'blk_1'=2,'blk_2'=8,'grp'=4] {'blk_1'}, dimensions={0}, use_global_device_ids=true | all-gather | bytes 3072 | tf_op jit(solution)/shard_map/all_gather | solution.py:22
  45.8 8.1 %all-gather.3 = s32[4,2,256]{2,1,0:T(2,128)S(1)} all-gather(s32[1,2,256]{2,1,0:T(2,128)S(1)} %copy.15), channel_id=1, replica_groups=mesh['blk_0'=4,'blk_1'=2,'blk_2'=8,'grp'=4] {'blk_0'}, dimensions={0}, use_global_device_ids=true | all-gather | bytes 10240 | tf_op jit(solution)/shard_map/all_gather | solution.py:22
  54.0 22.8 %all_gather.20 = s32[64,256]{1,0:T(8,128)S(1)} all-gather(s32[8,256]{1,0:T(8,128)S(1)} %reshape.76), channel_id=1, replica_groups=mesh['blk_0'=4,'blk_1'=2,'blk_2'=8,'grp'=4] {'blk_2'}, dimensions={0}, use_global_device_ids=true | all-gather | bytes 73728 | tf_op jit(solution)/shard_map/all_gather | solution.py:22
  76.8 64.4 %all-gather.9.cloned.1.call-done = bf16[64,256,256]{2,1,0:T(8,128)(2,1)} async-done(((bf16[8,256,256]{2,1,0:T(8,128)(2,1)}), bf16[64,256,256]{2,1,0:T(8,128)(2,1)}) %all-gather.9.cloned.1.call-update) | async-done | bytes 8388624 | tf_op jit(solution)/shard_map/all_gather | solution.py:22
  141.2 7.6 %copy.17 = bf16[4,2,8,256,256]{4,3,2,1,0:T(8,128)(2,1)} copy(bf16[4,2,8,256,256]{4,3,1,0,2:T(8,128)(2,1)} %bitcast.23) | data formatting | bytes 16777216 | tf_op jit(solution)/shard_map/transpose | solution.py:26
  148.8 0.0 copy-start.1
  148.8 0.0 copy-start.2
  148.8 0.0 copy-done
  148.8 28.2 %fusion.1 = (f32[1024]{0:T(1024)S(1)}, f32[1024,16384]{1,0:T(8,128)}) fusion(s32[16384]{0:T(1024)S(1)} %fusion.10, s32[16384]{0:T(1024)S(1)} %bitcast.26, s32[1024]{0:T(1024)} %param.6, s32[1024]{0:T(1024)} %param.7, bf16[1024,256]{1,0:T(8,128)(2,1)S(1)} %copy-done, bf16[16384,256]{1,0:T(8,128)(2,1)} %bitcast.24), kind=kOutput, calls=%fused_computation.5 | convolution fusion | flops 8690596864 | bytes 76165120 | tf_op jit(solution)/shard_map/dot_general | solution.py:75
  177.0 0.0 copy-done.1
  177.0 0.0 copy-done.2
  177.0 36.9 %select_reduce_fusion = (f32[1024]{0:T(1024)S(1)}, f32[1024]{0:T(1024)S(1)}) fusion(f32[1024,16384]{1,0:T(8,128)} %get-tuple-element.13, f32[1024]{0:T(1024)S(1)} %broadcast_maximum_fusion, s32[16384]{0:T(1024)S(1)} %fusion.10, s32[16384]{0:T(1024)S(1)} %bitcast.27, s32[1024]{0:T(1024)S(1)} %copy-done.1, s32[1024]{0:T(1024)S(1)} %copy-done.2), kind=kLoop, calls=%fused_computation.3 | loop fusion | flops 167770112 | bytes 67260416 | tf_op jit(solution)/shard_map/reduce_sum | solution.py:83
  214.0 9.7 %all_to_all.5 = f32[4,3,1024]{2,1,0:T(4,128)S(1)} all-to-all(f32[4,3,1024]{2,1,0:T(4,128)S(1)} %broadcast_in_dim.32), channel_id=1, replica_groups=mesh['blk_0'=4,'blk_1'=2,'blk_2'=8,'grp'=4] {'grp'}, dimensions={0} | all-to-all | bytes 98304 | tf_op jit(solution)/shard_map/all_to_all | solution.py:35
  223.9 0.6 fusion.12
  (20 shorter events, 0.4 us)
Async XLA Ops:
  6.5 142.3 %copy-start = (bf16[1024,256]{1,0:T(8,128)(2,1)S(1)}, bf16[1024,256]{1,0:T(8,128)(2,1)}, u32[]{:S(2)}) copy-start(bf16[1024,256]{1,0:T(8,128)(2,1)} %param.5) | copy-start | bytes 1572868
  6.5 35.9 %all-gather.7.cloned.1.call-start = ((), (), s32[]{:S(2)}) async-start(), calls=%async_computation.1 | async-start | bytes 1310720 | tf_op jit(solution)/shard_map/all_gather | solution.py:22
  13.7 127.6 %all-gather.9.cloned.1.call-start = ((), (), s32[]{:S(2)}) async-start(), calls=%async_computation.2 | async-start | bytes 9437184 | tf_op jit(solution)/shard_map/all_gather | solution.py:22
  148.8 28.2 %copy-start.1 = (s32[1024]{0:T(1024)S(1)}, s32[1024]{0:T(1024)}, u32[]{:S(2)}) copy-start(s32[1024]{0:T(1024)} %param.6) | copy-start | bytes 12292
  148.8 28.2 %copy-start.2 = (s32[1024]{0:T(1024)S(1)}, s32[1024]{0:T(1024)}, u32[]{:S(2)}) copy-start(s32[1024]{0:T(1024)} %param.7) | copy-start | bytes 12292
Sparse Core Ops, SparseCore 0:
  13.8 28.6 all-gather.6
  44.3 96.9 all-gather.8
where the time goes:
time: 232 us; the launch traced here: 231 us
  waiting for transfers between devices  93.2 us (40%)
  blocking collectives  51 us (22%)
  other arithmetic  37.6 us (16%)
  matrix products  28.2 us (12%)
  between operations  13.5 us (6%)
  local copies, waits for them, and re-layouts  7.94 us (3%)
    all_gather x2, waiting for transfers between devices, stacked_from(): parts = lax.all_gather(parts, axes[k], axis=0, tiled=True)  93.1 us
    all_gather x4, blocking collectives, stacked_from(): parts = lax.all_gather(parts, axes[k], axis=0, tiled=True)  41.3 us
    reduce_sum x1, other arithmetic, score_block(): totals = jnp.sum(weights, axis=1)  36.9 us
    dot_general x1, matrix products, score_block(): lax.dot_general(sources, block, (((1,), (1,)), ((), ())), preferred_eleme...  28.2 us
    all_to_all x1, blocking collectives, copy_for_each(): lax.all_to_all(jnp.broadcast_to(x[None], (size, *x.shape)), axis, 0, 0, t...  9.68 us
    transpose x1, local copies, waits for them, and re-layouts, stacked_from(): parts.transpose(*turned, *range(len(order), parts.ndim))  7.58 us
  transfers between devices with their start and end apart: 2, of which 2 were waited for; matrix products, arithmetic and copies ran while one was open for 0% of the time, Pallas kernels for 0%

commit v1 on v0

--- a/solution.py
+++ b/solution.py
@@ -10,6 +10,13 @@
 NEG = -1e30
 
 
+def gather_over(x, axis, dim):
+    peers = lax.axis_size(axis)
+    tiles = jnp.stack([x for _ in range(peers)])
+    tiles = lax.all_to_all(tiles, axis, split_axis=0, concat_axis=0)
+    return jnp.concatenate(tiles, axis=dim)
+
+
 def joined_along(parts, dim):
     dims = list(parts.shape[1:])
     dims[dim] *= parts.shape[0]
@@ -19,7 +26,7 @@
 def stacked_from(x, axes, order):
     parts = x[None]
     for k in order:
-        parts = lax.all_gather(parts, axes[k], axis=0, tiled=True)
+        parts = gather_over(parts, axes[k], 0)
     held = [lax.axis_size(axes[k]) for k in reversed(order)]
     parts = parts.reshape(*held, *x.shape)
     turned = sorted(range(len(order)), key=lambda place: order[len(order) - 1 - place])

time: 232 us -> 323 us (1.39)
  waiting for transfers between devices: 93.2 us -> 184 us
  between operations: 13.5 us -> 0.12 us
  starting transfers between devices: 0.04 us -> 13.1 us
  local copies, waits for them, and re-layouts: 7.94 us -> 12.8 us
    all_to_all x0 -> x2, waiting for transfers between devices: none -> 184 us  [gather_over(): tiles = lax.all_to_all(tiles, axis, split_axis=0, concat_axis=0)]
    all_gather x2 -> x0, waiting for transfers between devices: 93.1 us -> none  [stacked_from(): parts = lax.all_gather(parts, axes[k], axis=0, tiled=True)]
    all_gather x4 -> x0, blocking collectives: 41.3 us -> none  [stacked_from(): parts = lax.all_gather(parts, axes[k], axis=0, tiled=True)]
    all_to_all x0 -> x4, blocking collectives: none -> 32.3 us  [gather_over(): tiles = lax.all_to_all(tiles, axis, split_axis=0, concat_axis=0)]
    all_to_all x0 -> x2, starting transfers between devices: none -> 13.1 us  [gather_over(): tiles = lax.all_to_all(tiles, axis, split_axis=0, concat_axis=0)]
    all_to_all x1, blocking collectives: 9.68 us -> 18.3 us  [copy_for_each(): lax.all_to_all(jnp.broadcast_to(x[None], (size, *x.shape)), axis, 0, 0, t...]
    transpose x1 -> x0, local copies, waits for them, and re-layouts: 7.58 us -> none  [stacked_from(): parts.transpose(*turned, *range(len(order), parts.ndim))]
    all_to_all x0 -> x1, local copies, waits for them, and re-layouts: none -> 7.57 us  [gather_over(): tiles = lax.all_to_all(tiles, axis, split_axis=0, concat_axis=0)]
where the time goes in v1:
time: 323 us; the launch traced here: 322 us
  waiting for transfers between devices  184 us (57%)
  blocking collectives  50.7 us (16%)
  other arithmetic  36.2 us (11%)
  matrix products  25.4 us (8%)
  starting transfers between devices  13.1 us (4%)
  local copies, waits for them, and re-layouts  12.8 us (4%)
    all_to_all x2, waiting for transfers between devices, gather_over(): tiles = lax.all_to_all(tiles, axis, split_axis=0, concat_axis=0)  184 us
    reduce_sum x1, other arithmetic, score_block(): totals = jnp.sum(weights, axis=1)  33.8 us
    all_to_all x4, blocking collectives, gather_over(): tiles = lax.all_to_all(tiles, axis, split_axis=0, concat_axis=0)  32.3 us
    dot_general x1, matrix products, score_block(): lax.dot_general(sources, block, (((1,), (1,)), ((), ())), preferred_eleme...  25.4 us
    all_to_all x1, blocking collectives, copy_for_each(): lax.all_to_all(jnp.broadcast_to(x[None], (size, *x.shape)), axis, 0, 0, t...  18.3 us
    all_to_all x2, starting transfers between devices, gather_over(): tiles = lax.all_to_all(tiles, axis, split_axis=0, concat_axis=0)  13.1 us
    all_to_all x1, local copies, waits for them, and re-layouts, gather_over(): tiles = lax.all_to_all(tiles, axis, split_axis=0, concat_axis=0)  7.57 us
  transfers between devices with their start and end apart: 2, of which 2 were waited for; matrix products, arithmetic and copies ran while one was open for 0% of the time, Pallas kernels for 0%

profile of v1, /device:TPU:1, one launch (start us, length us, event | category | flops | bytes accessed | tf_op | source)
XLA Modules:
  0.0 322.5 jit_solution(648658534467998901)
XLA Ops:
  0.0 0.0 copy-start
  0.0 0.8 pad_add_fusion
  0.8 5.8 %all_to_all.35 = s32[2,1,256]{2,1,0:T(1,128)S(1)} all-to-all(s32[2,1,256]{2,1,0:T(1,128)S(1)} %pad_add_fusion), channel_id=1, replica_groups=mesh['blk_0'=4,'blk_1'=2,'blk_2'=8,'grp'=4] {'blk_1'}, dimensions={0} | all-to-all | bytes 4096 | tf_op jit(solution)/shard_map/all_to_all | solution.py:16
  6.6 8.0 %all_to_all.36 = s32[4,2,256]{2,1,0:T(2,128)S(1)} all-to-all(s32[4,2,256]{2,1,0:T(2,128)S(1)} %stack.19), channel_id=1, replica_groups=mesh['blk_0'=4,'blk_1'=2,'blk_2'=8,'grp'=4] {'blk_0'}, dimensions={0} | all-to-all | bytes 16384 | tf_op jit(solution)/shard_map/all_to_all | solution.py:16
  14.6 0.6 stack.20
  15.2 8.2 %all-to-all-start.2 = ((s32[8,8,256]{2,1,0:T(8,128)}), s32[8,8,256]{2,1,0:T(8,128)S(1)}, u32[]{:S(2)}, u32[]{:S(2)}) async-start(s32[8,8,256]{2,1,0:T(8,128)} %stack.20), calls=%async_computation.2 | async-start | bytes 131072 | tf_op jit(solution)/shard_map/all_to_all | solution.py:16
  23.4 1.0 pad_maximum_fusion
  24.4 6.2 %all-to-all-done.2 = s32[8,8,256]{2,1,0:T(8,128)S(1)} async-done(((s32[8,8,256]{2,1,0:T(8,128)}), s32[8,8,256]{2,1,0:T(8,128)S(1)}, u32[]{:S(2)}, u32[]{:S(2)}) %all-to-all-start.2) | async-done | bytes 65568 | tf_op jit(solution)/shard_map/all_to_all | solution.py:16
  30.6 6.4 %all_to_all.37 = bf16[2,1,256,256]{3,2,1,0:T(8,128)(2,1)S(1)} all-to-all(bf16[2,1,256,256]{3,2,1,0:T(8,128)(2,1)S(1)} %pad_maximum_fusion), channel_id=1, replica_groups=mesh['blk_0'=4,'blk_1'=2,'blk_2'=8,'grp'=4] {'blk_1'}, dimensions={0} | all-to-all | bytes 524288 | tf_op jit(solution)/shard_map/all_to_all | solution.py:16
  37.0 0.1 stack.22
  37.1 12.2 %all_to_all.38 = bf16[4,2,256,256]{3,2,1,0:T(8,128)(2,1)S(1)} all-to-all(bf16[4,2,256,256]{3,2,1,0:T(8,128)(2,1)S(1)} %stack.22), channel_id=1, replica_groups=mesh['blk_0'=4,'blk_1'=2,'blk_2'=8,'grp'=4] {'blk_0'}, dimensions={0} | all-to-all | bytes 2097152 | tf_op jit(solution)/shard_map/all_to_all | solution.py:16
  49.2 4.2 %stack.23 = bf16[8,8,256,256]{3,2,1,0:T(8,128)(2,1)} broadcast(bf16[8,256,256]{2,1,0:T(8,128)(2,1)S(1)} %bitcast.40), dimensions={1,2,3} | broadcast | bytes 9437184 | tf_op jit(solution)/shard_map/stack | solution.py:15
  53.5 4.9 %all-to-all-start.5 = ((bf16[8,8,256,256]{3,2,1,0:T(8,128)(2,1)}), bf16[8,8,256,256]{3,2,1,0:T(8,128)(2,1)}, u32[]{:S(2)}, u32[]{:S(2)}) async-start(bf16[8,8,256,256]{3,2,1,0:T(8,128)(2,1)} %stack.23), calls=%async_computation.5 | async-start | bytes 16777216 | tf_op jit(solution)/shard_map/all_to_all | solution.py:16
  58.5 177.8 %all-to-all-done.5 = bf16[8,8,256,256]{3,2,1,0:T(8,128)(2,1)} async-done(((bf16[8,8,256,256]{3,2,1,0:T(8,128)(2,1)}), bf16[8,8,256,256]{3,2,1,0:T(8,128)(2,1)}, u32[]{:S(2)}, u32[]{:S(2)}) %all-to-all-start.5) | async-done | bytes 8388640 | tf_op jit(solution)/shard_map/all_to_all | solution.py:16
  236.4 7.6 %copy.11 = bf16[8,8,256,256]{3,2,0,1:T(8,128)(2,1)} copy(bf16[8,8,256,256]{3,2,1,0:T(8,128)(2,1)} %all-to-all-done.5) | data formatting | bytes 16777216 | tf_op jit(solution)/shard_map/all_to_all | solution.py:16
  243.9 0.0 copy-done
  243.9 0.0 copy-start.1
  243.9 0.0 copy-start.2
  243.9 25.4 %fusion.1 = (f32[1024]{0:T(1024)S(1)}, f32[16384,1024]{1,0:T(8,128)}) fusion(s32[1024]{0:T(1024)} %param.6, s32[1024]{0:T(1024)} %param.7, s32[16384]{0:T(1024)S(1)} %fusion.10, s32[16384]{0:T(1024)S(1)} %bitcast.42, bf16[16384,256]{1,0:T(8,128)(2,1)} %bitcast.39, bf16[1024,256]{1,0:T(8,128)(2,1)S(1)} %copy-done), kind=kOutput, calls=%fused_computation.5 | convolution fusion | flops 8690596864 | bytes 76165120 | tf_op jit(solution)/shard_map/dot_general | solution.py:82
  269.4 0.0 copy-done.1
  269.4 0.0 copy-done.2
  269.4 33.8 %select_reduce_fusion = (f32[1024]{0:T(1024)S(1)}, f32[1024]{0:T(1024)S(1)}) fusion(f32[16384,1024]{1,0:T(8,128)} %get-tuple-element.13, f32[1024]{0:T(1024)S(1)} %broadcast_maximum_fusion, s32[1024]{0:T(1024)S(1)} %copy-done.1, s32[1024]{0:T(1024)S(1)} %copy-done.2, s32[16384]{0:T(1024)S(1)} %fusion.10, s32[16384]{0:T(1024)S(1)} %bitcast.43), kind=kLoop, calls=%fused_computation.4 | loop fusion | flops 167770112 | bytes 67260416 | tf_op jit(solution)/shard_map/reduce_sum | solution.py:90
  303.2 18.3 %all_to_all.39 = f32[4,3,1024]{2,1,0:T(4,128)S(1)} all-to-all(f32[4,3,1024]{2,1,0:T(4,128)S(1)} %broadcast_in_dim.24), channel_id=1, replica_groups=mesh['blk_0'=4,'blk_1'=2,'blk_2'=8,'grp'=4] {'grp'}, dimensions={0} | all-to-all | bytes 98304 | tf_op jit(solution)/shard_map/all_to_all | solution.py:42
  321.8 0.6 fusion.12
  (20 shorter events, 0.4 us)
Async XLA Ops:
  0.0 243.9 %copy-start = (bf16[1024,256]{1,0:T(8,128)(2,1)S(1)}, bf16[1024,256]{1,0:T(8,128)(2,1)}, u32[]{:S(2)}) copy-start(bf16[1024,256]{1,0:T(8,128)(2,1)} %param.5) | copy-start | bytes 1572868
  15.2 15.4 %all-to-all-start.2 = ((s32[8,8,256]{2,1,0:T(8,128)}), s32[8,8,256]{2,1,0:T(8,128)S(1)}, u32[]{:S(2)}, u32[]{:S(2)}) async-start(s32[8,8,256]{2,1,0:T(8,128)} %stack.20), calls=%async_computation.2 | async-start | bytes 131072 | tf_op jit(solution)/shard_map/all_to_all | solution.py:16
  53.5 182.9 %all-to-all-start.5 = ((bf16[8,8,256,256]{3,2,1,0:T(8,128)(2,1)}), bf16[8,8,256,256]{3,2,1,0:T(8,128)(2,1)}, u32[]{:S(2)}, u32[]{:S(2)}) async-start(bf16[8,8,256,256]{3,2,1,0:T(8,128)(2,1)} %stack.23), calls=%async_computation.5 | async-start | bytes 16777216 | tf_op jit(solution)/shard_map/all_to_all | solution.py:16
  243.9 25.5 %copy-start.1 = (s32[1024]{0:T(1024)S(1)}, s32[1024]{0:T(1024)}, u32[]{:S(2)}) copy-start(s32[1024]{0:T(1024)} %param.6) | copy-start | bytes 12292
  243.9 25.5 %copy-start.2 = (s32[1024]{0:T(1024)S(1)}, s32[1024]{0:T(1024)}, u32[]{:S(2)}) copy-start(s32[1024]{0:T(1024)} %param.7) | copy-start | bytes 12292
